TPU v7x, 32 devices: a whole 2x2x4 slice. The times are simulated.
32 devices in a mesh: grp: 4 (over z), row: 4 (over x, core), col: 2 (over y).
Axes of the slice: x: 2, y: 2, z: 4, core: 2. Of those that a mesh axis runs over, the one named last changes fastest.
Arguments:
- acts: bfloat16 [768, 8192], P('grp', 'col'), may hold values from -6 to 6
- grads: bfloat16 [768, 28672], P('grp', ('row', 'col')), may hold values from -6 to 6
- basis_in: bfloat16 [8192, 4096], P('col', 'row'), may hold values from -0.0625 to 0.0625
- basis_out: bfloat16 [4, 7168, 14336], P('row', 'grp', 'col'), may hold values from -0.03125 to 0.03125
- lengths: int32 [4, 2], P('grp'), may hold values from 1 to 96, 144 in all within a row
Outputs:
- eigenvalues: float32 [14336, 4096], P('col', 'row')
Inputs may be any that keep to these rules, and one draw needn't show every extreme that they name: The 2 lengths of each index of grp sum to exactly 144, and none exceeds 96.
All inputs are finite; a program needn't handle non-finite values.
Results may differ from a plain program's by a relative error of at most 0.006.
Values may be sent and summed in bfloat16 or wider, within the bound.
A program may use at most 256 MiB of HBM per device.

v0:
```python
import jax
import jax.numpy as jnp
from jax import lax
from jax.sharding import PartitionSpec as P

LEN = 96
VALID = 144


def outer_square(left, right):
    block = lax.dot_general(
        left, right, (((0,), (0,)), ((), ())), preferred_element_type=jnp.float32
    )
    return block * block


def per_device(acts, grads, basis_in, basis_out, lengths):
    seq_lens = lengths[0]
    count = seq_lens.shape[0]
    partial_in = jnp.dot(acts, basis_in, preferred_element_type=jnp.float32)
    proj_in = lax.psum(partial_in, "col").astype(jnp.bfloat16)
    ends = jnp.cumsum(seq_lens)
    starts = ends - seq_lens
    slot_ids = jnp.arange(VALID, dtype=jnp.int32)
    segment = jnp.sum((slot_ids[:, None] >= ends[None, :]).astype(jnp.int32), axis=1)
    member = segment[:, None] == jnp.arange(count, dtype=jnp.int32)[None, :]
    offset = jnp.sum(jnp.where(member, starts[None, :], 0), axis=1)
    source = segment * LEN + slot_ids - offset
    packed = jnp.take(grads, source, axis=0)
    gathered = lax.all_gather(packed, "col", axis=1, tiled=True)
    proj_in = jnp.take(proj_in, source, axis=0)
    partial_out = jnp.dot(
        gathered,
        lax.all_gather(basis_out, "grp", axis=1, tiled=True)[0],
        preferred_element_type=jnp.float32,
    )
    proj_out = lax.psum(partial_out, "row").astype(jnp.bfloat16)
    slot_pos = jnp.arange(LEN, dtype=jnp.int32)
    total = jnp.zeros((proj_out.shape[1], proj_in.shape[1]), jnp.float32)
    padded_out = jnp.concatenate(
        [proj_out, jnp.zeros((LEN, proj_out.shape[1]), jnp.bfloat16)], axis=0
    )
    padded_in = jnp.concatenate([proj_in, jnp.zeros((LEN, proj_in.shape[1]), jnp.bfloat16)], axis=0)
    for seq in range(count):
        keep = (slot_pos < seq_lens[seq]).astype(jnp.bfloat16)
        piece_out = lax.dynamic_slice_in_dim(padded_out, starts[seq], LEN, 0)
        piece_in = lax.dynamic_slice_in_dim(padded_in, starts[seq], LEN, 0)
        total = total + outer_square(piece_out * keep[:, None], piece_in)
    summed = lax.psum(total, "grp")
    return summed / (lax.axis_size("grp") * count * LEN)


def solution(mesh):
    in_specs = (
        P("grp", "col"),
        P("grp", ("row", "col")),
        P("col", "row"),
        P("row", "grp", "col"),
        P("grp", None),
    )
    out_specs = P("col", "row")
    return jax.shard_map(
        per_device, mesh=mesh, in_specs=in_specs, out_specs=out_specs, check_vma=False
    )
```

profile of v0, /device:TPU:0, one launch (start us, length us, event | category | flops | bytes accessed | tf_op | source)
XLA Modules:
  0.0 2906.0 jit_solution(11868883489751046661)
XLA Ops:
  6.5 0.0 copy-start
  6.5 0.0 all-gather.3.cloned.1.call-start
  6.5 0.9 reduce-window.4
  7.5 0.7 fusion.13
  8.1 0.1 fusion.9
  8.2 0.1 fusion.10
  8.4 3.7 gather_fusion
  12.1 1.1 broadcast_select_fusion
  13.2 0.0 all-gather.3.cloned.1.call-update
  13.3 0.0 copy-start.2
  13.3 0.0 all-gather.5.cloned.1.call-start
  13.3 0.7 all-gather.5.cloned.1.call-update
  14.0 0.0 all-reduce.6.cloned.1.call-start
  14.1 0.0 copy-done.2
  14.1 0.6 fusion.17
  17.1 0.0 copy-done
  17.1 5.2 fusion.18
  22.2 43.5 %all-reduce.8 = bf16[192,1024]{1,0:T(8,128)(2,1)S(1)} all-reduce(f32[192,1024]{1,0:T(8,128)S(1)} %fusion.18), channel_id=1, replica_groups=mesh['grp'=4,'row'=4,'col'=2] {'col'}, use_global_device_ids=true, to_apply=%region_4.5 | all-reduce | flops 196608 | bytes 1179648 | tf_op jit(solution)/shard_map/psum | solution.py:21
  65.7 0.9 gather_fusion.1
  67.8 0.6 fusion.16
  68.4 0.6 compare_convert_fusion.2
  69.0 0.6 compare_convert_fusion.1
  69.6 0.1 broadcast_select_fusion.1
  69.7 0.0 all-gather.3.cloned.1.call-done
  69.7 1693.3 %all-gather.5.cloned.1.call-done = bf16[1,7168,7168]{2,1,0:T(8,128)(2,1)} async-done(((bf16[1,1792,7168]{2,1,0:T(8,128)(2,1)}), bf16[1,7168,7168]{2,1,0:T(8,128)(2,1)}) %all-gather.5.cloned.1.call-update) | async-done | bytes 102760464 | tf_op jit(solution)/shard_map/all_gather | solution.py:34
  1763.0 37.1 %fusion = f32[144,7168]{1,0:T(8,128)} fusion(bf16[144,7168]{1,0:T(8,128)(2,1)} %all-gather.3.cloned.1.call-done, bf16[1,7168,7168]{2,1,0:T(8,128)(2,1)} %all-gather.5.cloned.1.call-done), kind=kOutput, calls=%fused_computation.2 | convolution fusion | flops 14797504512 | bytes 108953600 | tf_op jit(solution)/shard_map/dot_general | solution.py:32
  1800.1 76.2 %all-reduce.7 = bf16[144,7168]{1,0:T(8,128)(2,1)} all-reduce(f32[144,7168]{1,0:T(8,128)} %fusion), channel_id=1, replica_groups=mesh['grp'=4,'row'=4,'col'=2] {'row'}, use_global_device_ids=true, to_apply=%region_3.4 | all-reduce | flops 1032192 | bytes 6193152 | tf_op jit(solution)/shard_map/psum | solution.py:37
  1876.3 13.9 fusion.3
  1890.2 19.6 multiply_add_fusion
  1909.8 0.0 all-reduce.6.cloned.1.call-update
  1909.8 966.3 %all-reduce.6.cloned.1.call-done = f32[7168,1024]{1,0:T(8,128)} async-done(((f32[7168,1024]{1,0:T(8,128)}), f32[7168,1024]{1,0:T(8,128)}) %all-reduce.6.cloned.1.call-update) | async-done | bytes 29360144 | tf_op jit(solution)/shard_map/psum | solution.py:49
  2876.1 0.0 copy-start.1
  2876.1 23.3 broadcast_multiply_fusion
  2899.4 0.0 copy-done.1
  (5 shorter events, 0.0 us)
Async XLA Ops:
  6.5 10.5 copy-start
  6.5 63.2 %all-gather.3.cloned.1.call-start = ((), (), s32[]{:S(2)}) async-start(), calls=%async_computation | async-start | bytes 3096576 | tf_op jit(solution)/shard_map/all_gather | solution.py:30
  13.3 0.8 copy-start.2
  13.3 1749.7 %all-gather.5.cloned.1.call-start = ((), (), s32[]{:S(2)}) async-start(), calls=%async_computation.1 | async-start | bytes 128450560 | tf_op jit(solution)/shard_map/all_gather | solution.py:34
  14.0 2862.1 %all-reduce.6.cloned.1.call-start = ((), (), s32[]{:S(2)}) async-start(), calls=%async_computation.2 | async-start | bytes 58720256 | tf_op jit(solution)/shard_map/psum | solution.py:49
  2876.1 23.3 copy-start.1
Sparse Core Ops, SparseCore 0:
  13.4 52.2 all-gather.2
  67.3 1695.6 all-gather.4
  1909.9 966.1 all-reduce.5
where the time goes:
time: 2910 us
  waiting for transfers between devices  2660 us (91%)
  blocking collectives  120 us (4%)
  matrix products  75.7 us (3%)
    all_gather x1, waiting for transfers between devices, per_device(): lax.all_gather(basis_out, 'grp', axis=1, tiled=True)[0]  1690 us
    psum x1, waiting for transfers between devices, per_device(): summed = lax.psum(total, 'grp')  966 us
    psum x1, blocking collectives, per_device(): proj_out = lax.psum(partial_out, 'row').astype(jnp.bfloat16)  76.2 us
  transfers between devices with their start and end apart: 3, of which 2 were waited for; matrix products, arithmetic and copies ran while one was open for 0% of the time, Pallas kernels for 0%

commit v1 on v0

--- a/solution.py
+++ b/solution.py
@@ -31,7 +31,7 @@
     proj_in = jnp.take(proj_in, source, axis=0)
     partial_out = jnp.dot(
         gathered,
-        lax.all_gather(basis_out, "grp", axis=1, tiled=True)[0],
+        jnp.concatenate(lax.all_gather(basis_out, "grp"), axis=1)[0],
         preferred_element_type=jnp.float32,
     )
     proj_out = lax.psum(partial_out, "row").astype(jnp.bfloat16)

time: 2910 us -> 2910 us (level)
  no operation moved by 1% of the time
where the time goes in v1:
time: 2910 us
  waiting for transfers between devices  2660 us (91%)
  blocking collectives  120 us (4%)
  matrix products  75.7 us (3%)
    all_gather x1, waiting for transfers between devices, per_device(): lax.all_gather(basis_out, 'grp')  1690 us
    psum x1, waiting for transfers between devices, per_device(): summed = lax.psum(total, 'grp')  966 us
    psum x1, blocking collectives, per_device(): proj_out = lax.psum(partial_out, 'row').astype(jnp.bfloat16)  76.2 us
  transfers between devices with their start and end apart: 3, of which 2 were waited for; matrix products, arithmetic and copies ran while one was open for 0% of the time, Pallas kernels for 0%

profile of v1, /device:TPU:0, one launch (start us, length us, event | category | flops | bytes accessed | tf_op | source)
XLA Modules:
  0.0 2906.0 jit_solution(11868883489751046661)
XLA Ops:
  6.5 0.0 copy-start
  6.5 0.0 all-gather.4.cloned.1.call-start
  6.5 0.9 reduce-window.4
  7.5 0.7 fusion.11
  8.1 0.1 fusion.7
  8.2 0.1 fusion.8
  8.4 3.7 gather_fusion
  12.1 1.1 broadcast_select_fusion
  13.2 0.0 all-gather.4.cloned.1.call-update
  13.3 0.0 copy-start.2
  13.3 0.0 all-gather.6.cloned.1.call-start
  13.3 0.7 all-gather.6.cloned.1.call-update
  14.0 0.0 all-reduce.6.cloned.1.call-start
  14.1 0.0 copy-done.2
  14.1 0.6 fusion.15
  17.1 0.0 copy-done
  17.1 5.2 fusion.17
  22.2 43.5 %all-reduce.8 = bf16[192,1024]{1,0:T(8,128)(2,1)S(1)} all-reduce(f32[192,1024]{1,0:T(8,128)S(1)} %fusion.17), channel_id=1, replica_groups=mesh['grp'=4,'row'=4,'col'=2] {'col'}, use_global_device_ids=true, to_apply=%region_4.5 | all-reduce | flops 196608 | bytes 1179648 | tf_op jit(solution)/shard_map/psum | solution.py:21
  65.7 0.9 gather_fusion.1
  67.8 0.6 fusion.14
  68.4 0.6 compare_convert_fusion.2
  69.0 0.6 compare_convert_fusion.1
  69.6 0.1 broadcast_select_fusion.1
  69.7 0.0 all-gather.4.cloned.1.call-done
  69.7 1693.3 %all-gather.6.cloned.1.call-done = bf16[4,1792,7168]{2,1,0:T(8,128)(2,1)} async-done(((bf16[1,1792,7168]{2,1,0:T(8,128)(2,1)}), bf16[4,1792,7168]{2,1,0:T(8,128)(2,1)}) %all-gather.6.cloned.1.call-update) | async-done | bytes 102760464 | tf_op jit(solution)/shard_map/all_gather | solution.py:34
  1763.0 37.1 %fusion.16 = f32[144,7168]{1,0:T(8,128)} fusion(bf16[144,7168]{1,0:T(8,128)(2,1)} %all-gather.4.cloned.1.call-done, bf16[7168,7168]{1,0:T(8,128)(2,1)} %bitcast.7), kind=kOutput, calls=%fused_computation.35 | convolution fusion | flops 14797504512 | bytes 108953600 | tf_op jit(solution)/shard_map/dot_general | solution.py:32
  1800.1 76.2 %all-reduce.7 = bf16[144,7168]{1,0:T(8,128)(2,1)} all-reduce(f32[144,7168]{1,0:T(8,128)} %fusion.16), channel_id=1, replica_groups=mesh['grp'=4,'row'=4,'col'=2] {'row'}, use_global_device_ids=true, to_apply=%region_3.4 | all-reduce | flops 1032192 | bytes 6193152 | tf_op jit(solution)/shard_map/psum | solution.py:37
  1876.3 13.9 fusion.1
  1890.2 19.6 multiply_add_fusion
  1909.8 0.0 all-reduce.6.cloned.1.call-update
  1909.8 966.3 %all-reduce.6.cloned.1.call-done = f32[7168,1024]{1,0:T(8,128)} async-done(((f32[7168,1024]{1,0:T(8,128)}), f32[7168,1024]{1,0:T(8,128)}) %all-reduce.6.cloned.1.call-update) | async-done | bytes 29360144 | tf_op jit(solution)/shard_map/psum | solution.py:49
  2876.1 0.0 copy-start.1
  2876.1 23.3 broadcast_multiply_fusion
  2899.4 0.0 copy-done.1
  (5 shorter events, 0.0 us)
Async XLA Ops:
  6.5 10.5 copy-start
  6.5 63.2 %all-gather.4.cloned.1.call-start = ((), (), s32[]{:S(2)}) async-start(), calls=%async_computation | async-start | bytes 3096576 | tf_op jit(solution)/shard_map/all_gather | solution.py:30
  13.3 0.8 copy-start.2
  13.3 1749.7 %all-gather.6.cloned.1.call-start = ((), (), s32[]{:S(2)}) async-start(), calls=%async_computation.2 | async-start | bytes 128450560 | tf_op jit(solution)/shard_map/all_gather | solution.py:34
  14.0 2862.1 %all-reduce.6.cloned.1.call-start = ((), (), s32[]{:S(2)}) async-start(), calls=%async_computation.1 | async-start | bytes 58720256 | tf_op jit(solution)/shard_map/psum | solution.py:49
  2876.1 23.3 copy-start.1
Sparse Core Ops, SparseCore 0:
  13.4 52.2 all-gather.3
  67.3 1695.6 all-gather.5
  1909.9 966.1 all-reduce.5
